TPU v7x, 32 devices: a whole 2x2x4 slice. The times are simulated.
32 devices in a mesh: vocab: 32 (over z, y, x, core).
Axes of the slice: x: 2, y: 2, z: 4, core: 2. Of those that a mesh axis runs over, the one named last changes fastest.
Arguments:
- hidden: bfloat16 [2, 256, 3584], P(None, 'vocab'), may hold values from -256 to 256
- head_weight: bfloat16 [3584, 24576], P(None, 'vocab'), may hold values from -1 to 1
- teacher: bfloat16 [2, 256, 24576], P(None, None, 'vocab'), may hold values from 0 to 1
Outputs:
- token_loss: float32 [2, 256], P(None, 'vocab')
- hidden_grad: bfloat16 [2, 256, 3584], P(None, 'vocab')
- head_grad: bfloat16 [3584, 24576], P(None, 'vocab')
All inputs are finite; a program needn't handle non-finite values.
Results may differ from a plain program's by a relative error of at most 0.012.
Values may be sent and summed in bfloat16 or wider, within the bound.
A program may use at most 128 MiB of HBM per device.

v0:
```python
import jax
import jax.numpy as jnp
from jax import lax
from jax.sharding import PartitionSpec as P


def finish(logit_block, target_block):
    target_wide = target_block.astype(jnp.float32)
    teacher_mass = jnp.sum(target_wide, axis=-1)
    cross_term = jnp.sum(target_wide * logit_block, axis=-1)
    peak_logit = jnp.max(logit_block, axis=-1)
    peak_logit = lax.pmax(peak_logit, "vocab")
    exp_total = jnp.sum(jnp.exp(logit_block - peak_logit[..., None]), axis=-1)
    exp_total, teacher_mass, cross_term = lax.psum((exp_total, teacher_mass, cross_term), "vocab")
    log_norm = peak_logit + jnp.log(exp_total)
    token_loss = teacher_mass * log_norm - cross_term
    logit_grad = (
        teacher_mass[..., None] * jnp.exp(logit_block - log_norm[..., None]) - target_wide
    ).astype(jnp.bfloat16)
    return (token_loss, logit_grad)


def shards(hidden, head_weight, teacher):
    group_count, row_count, model_width = hidden.shape
    contract = (((1,), (1,)), ((), ()))
    shard_rows = lax.all_gather(hidden, "vocab", axis=1, tiled=True)
    logits = jnp.einsum("crd,dv->crv", shard_rows, head_weight, preferred_element_type=jnp.float32)
    token_loss, logit_grad = finish(logits, teacher)
    row_total = lax.axis_size("vocab") * (group_count * row_count)
    per_group = row_total // group_count
    owner_count = per_group // row_count
    grad_block = logit_grad
    grad_block = (
        grad_block.reshape(group_count, owner_count, row_count, -1)
        .transpose(1, 0, 2, 3)
        .reshape(row_total, -1)
    )
    summed = lax.psum_scatter(
        lax.dot_general(grad_block, head_weight, contract, preferred_element_type=jnp.float32),
        "vocab",
        scatter_dimension=0,
        tiled=True,
    )
    hidden_grad = summed.reshape(group_count, row_count, model_width).astype(jnp.bfloat16)
    weight_grad = jnp.zeros((model_width, head_weight.shape[1]), jnp.bfloat16)
    for group_index in range(group_count):
        product_term = lax.dot_general(
            shard_rows[group_index],
            logit_grad[group_index],
            (((0,), (0,)), ((), ())),
            preferred_element_type=jnp.float32,
        )
        weight_grad = (weight_grad.astype(jnp.float32) + product_term).astype(jnp.bfloat16)
    own_loss = lax.dynamic_slice_in_dim(
        token_loss, lax.axis_index("vocab") * row_count, row_count, 1
    )
    return (own_loss, hidden_grad, weight_grad)


def solution(mesh):
    in_specs = (P(None, "vocab", None), P(None, "vocab"), P(None, None, "vocab"))
    out_specs = (P(None, "vocab"), P(None, "vocab", None), P(None, "vocab"))
    return jax.shard_map(shards, mesh=mesh, in_specs=in_specs, out_specs=out_specs, check_vma=False)
```

profile of v0, /device:TPU:0, one launch (start us, length us, event | category | flops | bytes accessed | tf_op | source)
XLA Modules:
  0.0 325.6 jit_solution(7871215503381196824)
XLA Ops:
  7.2 0.0 all-gather.2.cloned.1.call-start
  7.2 0.7 all-gather.2.cloned.1.call-update
  7.9 0.0 copy-start.1
  7.9 0.0 reduce-scatter.2.cloned.1.call-start
  8.0 66.4 %all-gather.2.cloned.1.call-done = bf16[2,256,3584]{2,1,0:T(8,128)(2,1)} async-done(((bf16[2,8,3584]{2,1,0:T(8,128)(2,1)}), bf16[2,256,3584]{2,1,0:T(8,128)(2,1)}) %all-gather.2.cloned.1.call-update) | async-done | bytes 3670032 | tf_op jit(solution)/shard_map/all_gather | solution.py:26
  74.3 6.8 %fusion.5 = (f32[2,256]{1,0:T(2,128)S(1)}, f32[2,256,768]{2,1,0:T(8,128)S(1)}) fusion(bf16[2,256,3584]{2,1,0:T(8,128)(2,1)} %all-gather.2.cloned.1.call-done, bf16[3584,768]{1,0:T(8,128)(2,1)} %param.4), kind=kOutput, calls=%fused_computation.19 | convolution fusion | flops 2818964992 | bytes 10749952 | tf_op jit(solution)/shard_map/crd,dv->crv/dot_general | solution.py:27
  81.1 38.5 %pmax.7 = f32[2,256]{1,0:T(2,128)S(1)} all-reduce(f32[2,256]{1,0:T(2,128)S(1)} %get-tuple-element.15), channel_id=1, replica_groups=mesh['vocab'=32] {'vocab'}, use_global_device_ids=true, to_apply=%region_3.0 | all-reduce | flops 512 | bytes 4096 | tf_op jit(solution)/shard_map/pmax | solution.py:12
  119.6 0.0 copy-done.1
  119.6 0.7 exponential_reduce_fusion
  120.4 40.7 %all-reduce = (f32[2,256]{1,0:T(2,128)S(1)}, f32[2,256]{1,0:T(2,128)S(1)}, f32[2,256]{1,0:T(2,128)S(1)}) all-reduce(f32[2,256]{1,0:T(2,128)S(1)} %get-tuple-element.10, f32[2,256]{1,0:T(2,128)S(1)} %get-tuple-element.9, f32[2,256]{1,0:T(2,128)S(1)} %get-tuple-element.11), channel_id=1, replica_groups=mesh['vocab'=32] {'vocab'}, use_global_device_ids=true, to_apply=%region_7.0 | all-reduce | flops 1536 | bytes 12288 | tf_op jit(solution)/shard_map/psum | solution.py:14
  161.0 0.4 fusion.4
  161.5 0.1 copy.7
  161.5 7.7 %fusion.6 = f32[512,3584]{1,0:T(8,128)} fusion(bf16[512,768]{1,0:T(8,128)(2,1)S(1)} %bitcast.29, bf16[3584,768]{1,0:T(8,128)(2,1)} %param.4), kind=kOutput, calls=%fused_computation.20 | convolution fusion | flops 2818572288 | bytes 13631488 | tf_op jit(solution)/shard_map/dot_general | solution.py:39
  169.2 0.0 reduce-scatter.2.cloned.1.call-update
  169.3 0.0 copy-start
  169.3 3.3 %convolution_convert_fusion = bf16[768,3584]{1,0:T(8,128)(2,1)S(1)} fusion(bf16[2,256,3584]{2,1,0:T(8,128)(2,1)} %all-gather.2.cloned.1.call-done, bf16[2,256,768]{2,1,0:T(8,128)(2,1)S(1)} %fusion.4), kind=kOutput, calls=%fused_computation.1 | convolution fusion | flops 1412038656 | bytes 7733248 | tf_op jit(solution)/shard_map/dot_general | solution.py:47
  172.6 0.0 copy-done
  172.6 4.0 %fusion = bf16[3584,768]{0,1:T(8,128)(2,1)} fusion(bf16[768,3584]{1,0:T(8,128)(2,1)S(1)} %convolution_convert_fusion, bf16[2,256,3584]{2,1,0:T(8,128)(2,1)S(1)} %copy-done, bf16[2,256,768]{2,1,0:T(8,128)(2,1)S(1)} %fusion.4), kind=kOutput, calls=%fused_computation.2 | convolution fusion | flops 1417543680 | bytes 13238272 | tf_op jit(solution)/shard_map/dot_general | solution.py:47
  176.6 8.3 %copy.8 = bf16[3584,768]{1,0:T(8,128)(2,1)} copy(bf16[3584,768]{0,1:T(8,128)(2,1)} %fusion) | data formatting | bytes 11010048
  184.9 0.6 dynamic-slice_subtract_fusion
  185.5 131.7 %reduce-scatter.2.cloned.1.call-done = f32[16,3584]{1,0:T(8,128)} async-done(((f32[512,3584]{1,0:T(8,128)}), f32[16,3584]{1,0:T(8,128)}) %reduce-scatter.2.cloned.1.call-update) | async-done | bytes 229392 | tf_op jit(solution)/shard_map/reduce_scatter | solution.py:38
  317.2 1.6 convert_bitcast_fusion
  (1 shorter events, 0.0 us)
Async XLA Ops:
  7.2 67.2 %all-gather.2.cloned.1.call-start = ((), (), s32[]{:S(2)}) async-start(), calls=%async_computation.1 | async-start | bytes 3784704 | tf_op jit(solution)/shard_map/all_gather | solution.py:26
  7.9 111.7 %copy-start.1 = (bf16[2,256,768]{2,1,0:T(8,128)(2,1)S(1)}, bf16[2,256,768]{2,1,0:T(8,128)(2,1)}, u32[]{:S(2)}) copy-start(bf16[2,256,768]{2,1,0:T(8,128)(2,1)} %param.5) | copy-start | bytes 2359300
  7.9 309.3 %reduce-scatter.2.cloned.1.call-start = ((), (), s32[]{:S(2)}) async-start(), calls=%async_computation.2 | async-start | bytes 7569408 | tf_op jit(solution)/shard_map/reduce_scatter | solution.py:38
  169.3 3.3 %copy-start = (bf16[2,256,3584]{2,1,0:T(8,128)(2,1)S(1)}, bf16[2,256,3584]{2,1,0:T(8,128)(2,1)}, u32[]{:S(2)}) copy-start(bf16[2,256,3584]{2,1,0:T(8,128)(2,1)} %all-gather.2.cloned.1.call-done) | copy-start | bytes 11010052
Sparse Core Ops, SparseCore 0:
  10.9 63.4 all-gather.1
  169.4 147.7 reduce-scatter.1
where the time goes:
time: 326 us
  waiting for transfers between devices  199 us (61%)
  blocking collectives  79.2 us (24%)
  matrix products  21.8 us (7%)
  between operations  14.1 us (4%)
  local copies, waits for them, and re-layouts  8.33 us (3%)
  other arithmetic  3.38 us (1%)
    reduce_scatter x1, waiting for transfers between devices, shards(): lax.psum_scatter(lax.dot_general(grad_block, head_weight, contract, prefe...  132 us
    all_gather x1, waiting for transfers between devices, shards(): shard_rows = lax.all_gather(hidden, 'vocab', axis=1, tiled=True)  66.4 us
    psum x1, blocking collectives, finish(): lax.psum((exp_total, teacher_mass, cross_term), 'vocab')  40.7 us
    pmax x1, blocking collectives, finish(): peak_logit = lax.pmax(peak_logit, 'vocab')  38.5 us
    unnamed x5, local copies, waits for them, and re-layouts  8.28 us
    dot_general x1, matrix products, shards(): lax.dot_general(grad_block, head_weight, contract, preferred_element_type...  7.71 us
    dot_general x2, matrix products, shards(): lax.dot_general(shard_rows[group_index], logit_grad[group_index], (((0,),...  7.29 us
    dot_general x1, matrix products, shards(): jnp.einsum('crd,dv->crv', shard_rows, head_weight, preferred_element_type...  6.76 us
  transfers between devices with their start and end apart: 2, of which 2 were waited for; matrix products, arithmetic and copies ran while one was open for 5% of the time, Pallas kernels for 0%

commit v1 on v0

--- a/solution.py
+++ b/solution.py
@@ -23,7 +23,9 @@
 def shards(hidden, head_weight, teacher):
     group_count, row_count, model_width = hidden.shape
     contract = (((1,), (1,)), ((), ()))
-    shard_rows = lax.all_gather(hidden, "vocab", axis=1, tiled=True)
+    shard_rows = jnp.concatenate(
+        lax.all_to_all(jnp.stack([hidden] * lax.axis_size("vocab")), "vocab", 0, 0), axis=1
+    )
     logits = jnp.einsum("crd,dv->crv", shard_rows, head_weight, preferred_element_type=jnp.float32)
     token_loss, logit_grad = finish(logits, teacher)
     row_total = lax.axis_size("vocab") * (group_count * row_count)

time: 326 us -> 347 us (1.064)
  blocking collectives: 79.2 us -> 169 us
  waiting for transfers between devices: 199 us -> 132 us
  matrix products: 21.8 us -> 18 us
    all_to_all x0 -> x1, blocking collectives: none -> 90.2 us  [shards(): lax.all_to_all(jnp.stack([hidden] * lax.axis_size('vocab')), 'vocab', 0, 0)]
    all_gather x1 -> x0, waiting for transfers between devices: 66.4 us -> none  [shards(): shard_rows = lax.all_gather(hidden, 'vocab', axis=1, tiled=True)]
    dot_general x1, matrix products: 6.76 us -> 3.1 us  [shards(): jnp.einsum('crd,dv->crv', shard_rows, head_weight, preferred_element_type...]
    unnamed x5 -> x9, local copies, waits for them, and re-layouts: 8.28 us -> 8.29 us
  transfers between devices with their start and end apart: 2 -> 1, of which waited for: 2 -> 1; matrix products, arithmetic and copies ran while one was open for 5% -> 5% of each run, Pallas kernels for 0% -> 0%
where the time goes in v1:
time: 347 us; the launch traced here: 346 us
  blocking collectives  169 us (49%)
  waiting for transfers between devices  132 us (38%)
  matrix products  18 us (5%)
  between operations  14.1 us (4%)
  local copies, waits for them, and re-layouts  9.64 us (3%)
    reduce_scatter x1, waiting for transfers between devices, shards(): lax.psum_scatter(lax.dot_general(grad_block, head_weight, contract, prefe...  132 us
    all_to_all x1, blocking collectives, shards(): lax.all_to_all(jnp.stack([hidden] * lax.axis_size('vocab')), 'vocab', 0, 0)  90.2 us
    psum x1, blocking collectives, finish(): lax.psum((exp_total, teacher_mass, cross_term), 'vocab')  40 us
    pmax x1, blocking collectives, finish(): peak_logit = lax.pmax(peak_logit, 'vocab')  38.9 us
    unnamed x9, local copies, waits for them, and re-layouts  8.29 us
    dot_general x1, matrix products, shards(): lax.dot_general(grad_block, head_weight, contract, preferred_element_type...  7.68 us
    dot_general x2, matrix products, shards(): lax.dot_general(shard_rows[group_index], logit_grad[group_index], (((0,),...  7.26 us
  transfers between devices with their start and end apart: 1, of which 1 were waited for; matrix products, arithmetic and copies ran while one was open for 5% of the time, Pallas kernels for 0%

profile of v1, /device:TPU:0, one launch (start us, length us, event | category | flops | bytes accessed | tf_op | source)
XLA Modules:
  0.0 346.4 jit_solution(2088082305554224112)
XLA Ops:
  7.2 0.0 reduce-scatter.2.cloned.1.call-start
  7.2 1.3 stack.2
  8.5 0.0 copy-start.3
  8.5 90.2 %all_to_all.5 = bf16[32,2,8,3584]{3,2,1,0:T(8,128)(2,1)S(1)} all-to-all(bf16[32,2,8,3584]{3,2,1,0:T(8,128)(2,1)S(1)} %stack.2), channel_id=1, replica_groups=mesh['vocab'=32] {'vocab'}, dimensions={0} | all-to-all | bytes 7340032 | tf_op jit(solution)/shard_map/all_to_all | solution.py:27
  98.7 0.0 copy-done.3
  98.7 0.0 copy-start
  98.7 3.1 fusion.7
  101.8 0.0 copy-done
  101.8 38.9 %pmax.7 = f32[2,256]{1,0:T(2,128)S(1)} all-reduce(f32[2,256]{1,0:T(2,128)S(1)} %get-tuple-element.18), channel_id=1, replica_groups=mesh['vocab'=32] {'vocab'}, use_global_device_ids=true, to_apply=%region_3.0 | all-reduce | flops 512 | bytes 4096 | tf_op jit(solution)/shard_map/pmax | solution.py:12
  140.7 0.0 copy-done.2
  140.7 0.7 exponential_reduce_fusion
  141.4 40.0 %all-reduce = (f32[2,256]{1,0:T(2,128)S(1)}, f32[2,256]{1,0:T(2,128)S(1)}, f32[2,256]{1,0:T(2,128)S(1)}) all-reduce(f32[2,256]{1,0:T(2,128)S(1)} %get-tuple-element.13, f32[2,256]{1,0:T(2,128)S(1)} %get-tuple-element.12, f32[2,256]{1,0:T(2,128)S(1)} %get-tuple-element.14), channel_id=1, replica_groups=mesh['vocab'=32] {'vocab'}, use_global_device_ids=true, to_apply=%region_7.0 | all-reduce | flops 1536 | bytes 12288 | tf_op jit(solution)/shard_map/psum | solution.py:14
  181.5 0.4 fusion.6
  181.9 0.1 copy.10
  181.9 7.7 %fusion.8 = f32[512,3584]{1,0:T(8,128)} fusion(bf16[512,768]{1,0:T(8,128)(2,1)S(1)} %bitcast.39, bf16[3584,768]{1,0:T(8,128)(2,1)} %param.4), kind=kOutput, calls=%fused_computation.22 | convolution fusion | flops 2818572288 | bytes 13631488 | tf_op jit(solution)/shard_map/dot_general | solution.py:41
  189.6 0.0 reduce-scatter.2.cloned.1.call-update
  189.7 0.0 copy-start.1
  189.7 3.3 convolution_convert_fusion
  192.9 0.0 copy-done.1
  192.9 4.0 %fusion = bf16[3584,768]{0,1:T(8,128)(2,1)} fusion(bf16[768,3584]{1,0:T(8,128)(2,1)S(1)} %convolution_convert_fusion, bf16[2,32,8,3584]{3,2,0,1:T(8,128)(2,1)S(1)} %bitcast.37, bf16[2,256,768]{2,1,0:T(8,128)(2,1)S(1)} %fusion.6), kind=kOutput, calls=%fused_computation.2 | convolution fusion | flops 1417543680 | bytes 13238272 | tf_op jit(solution)/shard_map/dot_general | solution.py:49
  196.9 8.3 %copy.11 = bf16[3584,768]{1,0:T(8,128)(2,1)} copy(bf16[3584,768]{0,1:T(8,128)(2,1)} %fusion) | data formatting | bytes 11010048
  205.2 0.6 dynamic-slice_subtract_fusion
  205.8 132.1 %reduce-scatter.2.cloned.1.call-done = f32[16,3584]{1,0:T(8,128)} async-done(((f32[512,3584]{1,0:T(8,128)}), f32[16,3584]{1,0:T(8,128)}) %reduce-scatter.2.cloned.1.call-update) | async-done | bytes 229392 | tf_op jit(solution)/shard_map/reduce_scatter | solution.py:40
  338.0 1.6 convert_bitcast_fusion
  (2 shorter events, 0.0 us)
Async XLA Ops:
  7.2 330.8 %reduce-scatter.2.cloned.1.call-start = ((), (), s32[]{:S(2)}) async-start(), calls=%async_computation.2 | async-start | bytes 7569408 | tf_op jit(solution)/shard_map/reduce_scatter | solution.py:40
  8.5 90.2 %copy-start.3 = (bf16[3584,768]{1,0:T(8,128)(2,1)S(1)}, bf16[3584,768]{1,0:T(8,128)(2,1)}, u32[]{:S(2)}) copy-start(bf16[3584,768]{1,0:T(8,128)(2,1)} %param.4) | copy-start | bytes 16515076
  98.7 3.1 copy-start
  98.7 42.0 %copy-start.2 = (bf16[2,256,768]{2,1,0:T(8,128)(2,1)S(1)}, bf16[2,256,768]{2,1,0:T(8,128)(2,1)}, u32[]{:S(2)}) copy-start(bf16[2,256,768]{2,1,0:T(8,128)(2,1)} %param.5) | copy-start | bytes 2359300
  189.7 3.3 copy-start.1
Sparse Core Ops, SparseCore 0:
  189.8 148.1 reduce-scatter.1
